TPU v7x, 32 devices: a whole 2x2x4 slice. The times are simulated.
32 devices in a mesh: dp: 4 (over y, x), seq: 8 (over z, core).
Axes of the slice: x: 2, y: 2, z: 4, core: 2. Of those that a mesh axis runs over, the one named last changes fastest.
Arguments:
- queries: bfloat16 [4, 1024, 2048], P('dp', 'seq'), may hold values from -6 to 6
- key_vectors: bfloat16 [4, 1024, 2048], P('dp', 'seq'), may hold values from -6 to 6
- values: bfloat16 [4, 1024, 2048], P('dp', 'seq'), may hold values from -6 to 6
- out_grad: bfloat16 [4, 1024, 2048], P('dp', 'seq'), may hold values from -6 to 6
- inputs: bfloat16 [4, 1024, 2048], P('dp', 'seq'), may hold values from -6 to 6
Outputs:
- query_grad: bfloat16 [4, 1024, 2048], P('dp', 'seq')
- key_grad: bfloat16 [4, 1024, 2048], P('dp', 'seq')
- value_grad: bfloat16 [4, 1024, 2048], P('dp', 'seq')
- weight_grad: float32 [2048, 2048], P('dp', 'seq')
All inputs are finite; a program needn't handle non-finite values.
Results may differ from a plain program's by a relative error of at most 0.025.
Values may be sent and summed in bfloat16 or wider, within the bound.
No kernel may reach another device: no remote copies, remote signals or barrier semaphores. Data moves between devices by JAX's collectives and lax.ppermute only.
A program may use at most 128 MiB of HBM per device.

v0:
```python
import jax
import jax.numpy as jnp
from jax import lax
from jax.sharding import PartitionSpec as P

HD = 128


def partner(value, axis, apart):
    return lax.ppermute(value, axis, [(i, i ^ 1 << apart) for i in range(lax.axis_size(axis))])


def body(queries, key_vectors, values, out_grad, inputs):
    seq_count = lax.axis_size("seq")
    groups = seq_count // 2
    parity = lax.axis_index("seq") % 2
    is_even = parity == 0
    tok_rows = queries.shape[1]
    half_rows = tok_rows // 2
    width = queries.shape[2]
    group_width = 2 * width // seq_count
    heads_here = group_width // HD
    model_width = inputs.shape[2]
    own_rows = seq_count * half_rows
    length = 2 * own_rows
    doc_rows = own_rows // 4
    block_rows = min(doc_rows, max(256, length // 16))
    block_count = own_rows // block_rows
    scale = HD ** (-0.5)

    def to_heads(array):
        return (
            array[0]
            .reshape(half_rows, 2, groups, group_width)
            .transpose(0, 2, 1, 3)
            .reshape(half_rows, seq_count, group_width)
        )

    moved = (
        lax.all_to_all(to_heads(queries), "seq", split_axis=1, concat_axis=0, tiled=True),
        lax.all_to_all(to_heads(key_vectors), "seq", split_axis=1, concat_axis=0, tiled=True),
        lax.all_to_all(to_heads(values), "seq", split_axis=1, concat_axis=0, tiled=True),
        lax.all_to_all(to_heads(out_grad), "seq", split_axis=1, concat_axis=0, tiled=True),
    )
    q_rows = moved[0].reshape(own_rows, group_width)
    k_rows = moved[1].reshape(own_rows, group_width)
    v_rows = moved[2].reshape(own_rows, group_width)
    g_rows = moved[3].reshape(own_rows, group_width)
    k_other, v_other = partner((k_rows, v_rows), "seq", 0)

    def in_order(mine, theirs):
        even_rows = jnp.where(is_even, mine, theirs)
        odd_rows = jnp.where(is_even, theirs, mine)
        return jnp.stack([even_rows, odd_rows], axis=1).reshape(2 * mine.shape[0], mine.shape[1])

    key_all = in_order(k_rows, k_other).reshape(length, heads_here, HD)
    value_all = in_order(v_rows, v_other).reshape(length, heads_here, HD)
    query_heads = q_rows.reshape(own_rows, heads_here, HD)
    grad_heads = g_rows.reshape(own_rows, heads_here, HD)
    key_total = jnp.zeros((length, heads_here, HD), jnp.float32)
    value_total = jnp.zeros((length, heads_here, HD), jnp.float32)
    query_parts = []
    for block in range(block_count):
        start = block * block_rows
        stop = start + block_rows
        low = 2 * (start // doc_rows * doc_rows)
        high = 2 * stop
        query_block = query_heads[start:stop]
        grad_block = grad_heads[start:stop]
        key_block = key_all[low:high]
        value_block = value_all[low:high]
        scores = (
            jnp.einsum("qhd,khd->hqk", query_block, key_block, preferred_element_type=jnp.float32)
            * scale
        )
        query_pos = 2 * (start + jnp.arange(block_rows, dtype=jnp.int32)) + parity
        key_pos = low + jnp.arange(high - low, dtype=jnp.int32)
        visible = key_pos[None, :] <= query_pos[:, None]
        scores = jnp.where(visible[None], scores, -jnp.inf)
        top = jnp.max(scores, axis=2, keepdims=True)
        weights = jnp.exp(scores - top)
        probs = weights / jnp.sum(weights, axis=2, keepdims=True)
        probs_low = probs.astype(jnp.bfloat16)
        dprob = jnp.einsum(
            "qhd,khd->hqk", grad_block, value_block, preferred_element_type=jnp.float32
        )
        delta = jnp.sum(probs * dprob, axis=2, keepdims=True)
        dscore = (probs * (dprob - delta) * scale).astype(jnp.bfloat16)
        query_parts.append(
            jnp.einsum(
                "hqk,khd->qhd", dscore, key_block, preferred_element_type=jnp.float32
            ).astype(jnp.bfloat16)
        )
        key_total = key_total.at[low:high].add(
            jnp.einsum("hqk,qhd->khd", dscore, query_block, preferred_element_type=jnp.float32)
        )
        value_total = value_total.at[low:high].add(
            jnp.einsum("hqk,qhd->khd", probs_low, grad_block, preferred_element_type=jnp.float32)
        )
    query_grad = jnp.concatenate(query_parts, axis=0).reshape(own_rows, group_width)

    def by_parity(total):
        paired = total.reshape(own_rows, 2, group_width)
        mine = jnp.where(is_even, paired[:, 0], paired[:, 1])
        theirs = jnp.where(is_even, paired[:, 1], paired[:, 0])
        return (mine.astype(jnp.bfloat16), theirs.astype(jnp.bfloat16))

    key_mine, key_theirs = by_parity(key_total)
    value_mine, value_theirs = by_parity(value_total)
    key_back, value_back = partner((key_theirs, value_theirs), "seq", 0)
    key_grad = (key_mine.astype(jnp.float32) + key_back.astype(jnp.float32)).astype(jnp.bfloat16)
    value_grad = (value_mine.astype(jnp.float32) + value_back.astype(jnp.float32)).astype(
        jnp.bfloat16
    )
    spread = jnp.broadcast_to(
        inputs[0].reshape(half_rows, 1, 2, model_width), (half_rows, groups, 2, model_width)
    ).reshape(half_rows, seq_count, model_width)
    input_rows = lax.all_to_all(spread, "seq", split_axis=1, concat_axis=0, tiled=True).reshape(
        own_rows, model_width
    )
    term = jnp.einsum("td,tc->dc", input_rows, value_grad, preferred_element_type=jnp.float32)
    halves = term.reshape(term.shape[0], 2, term.shape[1] // 2)
    mine = jnp.where(is_even, halves[:, 0], halves[:, 1])
    theirs = jnp.where(is_even, halves[:, 1], halves[:, 0])
    mine, theirs = (mine, theirs)
    received = partner(theirs.astype(jnp.bfloat16), "seq", 0).astype(theirs.dtype)
    weight_grad = lax.psum_scatter(
        (mine + received).astype(jnp.bfloat16), "dp", scatter_dimension=0, tiled=True
    ).astype(jnp.float32)

    def to_tokens(array):
        return array.reshape(seq_count, half_rows, 1, group_width)

    def from_heads(array):
        return (
            array.reshape(half_rows, groups, 2, group_width)
            .transpose(0, 2, 1, 3)
            .reshape(1, tok_rows, width)
        )

    returned = (
        lax.all_to_all(to_tokens(query_grad), "seq", split_axis=0, concat_axis=2, tiled=True),
        lax.all_to_all(to_tokens(key_grad), "seq", split_axis=0, concat_axis=2, tiled=True),
        lax.all_to_all(to_tokens(value_grad), "seq", split_axis=0, concat_axis=2, tiled=True),
    )
    return (from_heads(returned[0]), from_heads(returned[1]), from_heads(returned[2]), weight_grad)


def solution(mesh):
    return jax.shard_map(
        body,
        mesh=mesh,
        in_specs=(
            P("dp", "seq", None),
            P("dp", "seq", None),
            P("dp", "seq", None),
            P("dp", "seq", None),
            P("dp", "seq", None),
        ),
        out_specs=(
            P("dp", "seq", None),
            P("dp", "seq", None),
            P("dp", "seq", None),
            P("dp", "seq"),
        ),
        check_vma=False,
    )
```

profile of v0, /device:TPU:0, one launch (start us, length us, event | category | flops | bytes accessed | tf_op | source)
XLA Modules:
  0.0 255.6 jit_solution(17739342030090548654)
XLA Ops:
  9.6 6.5 %all-to-all-start.2 = ((bf16[64,8,512]{2,0,1:T(8,128)(2,1)}), bf16[64,8,512]{2,0,1:T(8,128)(2,1)S(1)}, u32[]{:S(2)}, u32[]{:S(2)}) async-start(bf16[64,8,512]{2,0,1:T(8,128)(2,1)} %bitcast.15), calls=%async_computation.2 | async-start | bytes 1048576 | tf_op jit(solution)/shard_map/all_to_all | solution.py:42
  17.4 14.0 %all-to-all-done.2 = bf16[64,8,512]{2,0,1:T(8,128)(2,1)S(1)} async-done(((bf16[64,8,512]{2,0,1:T(8,128)(2,1)}), bf16[64,8,512]{2,0,1:T(8,128)(2,1)S(1)}, u32[]{:S(2)}, u32[]{:S(2)}) %all-to-all-start.2) | async-done | bytes 524320 | tf_op jit(solution)/shard_map/all_to_all | solution.py:42
  31.4 3.6 %all-to-all-start.3 = ((bf16[64,8,512]{2,0,1:T(8,128)(2,1)}), bf16[64,8,512]{2,0,1:T(8,128)(2,1)S(1)}, u32[]{:S(2)}, u32[]{:S(2)}) async-start(bf16[64,8,512]{2,0,1:T(8,128)(2,1)} %bitcast.24), calls=%async_computation.3 | async-start | bytes 1048576 | tf_op jit(solution)/shard_map/all_to_all | solution.py:43
  36.4 13.9 %all-to-all-done.3 = bf16[64,8,512]{2,0,1:T(8,128)(2,1)S(1)} async-done(((bf16[64,8,512]{2,0,1:T(8,128)(2,1)}), bf16[64,8,512]{2,0,1:T(8,128)(2,1)S(1)}, u32[]{:S(2)}, u32[]{:S(2)}) %all-to-all-start.3) | async-done | bytes 524320 | tf_op jit(solution)/shard_map/all_to_all | solution.py:43
  50.4 3.5 %all-to-all-start = ((bf16[64,8,512]{2,0,1:T(8,128)(2,1)}), bf16[64,8,512]{2,0,1:T(8,128)(2,1)S(1)}, u32[]{:S(2)}, u32[]{:S(2)}) async-start(bf16[64,8,512]{2,0,1:T(8,128)(2,1)} %bitcast.1), calls=%async_computation | async-start | bytes 1048576 | tf_op jit(solution)/shard_map/all_to_all | solution.py:41
  55.9 13.2 %all-to-all-done = bf16[64,8,512]{2,0,1:T(8,128)(2,1)S(1)} async-done(((bf16[64,8,512]{2,0,1:T(8,128)(2,1)}), bf16[64,8,512]{2,0,1:T(8,128)(2,1)S(1)}, u32[]{:S(2)}, u32[]{:S(2)}) %all-to-all-start) | async-done | bytes 524320 | tf_op jit(solution)/shard_map/all_to_all | solution.py:41
  69.1 3.5 %all-to-all-start.1 = ((bf16[64,8,512]{2,0,1:T(8,128)(2,1)}), bf16[64,8,512]{2,0,1:T(8,128)(2,1)S(1)}, u32[]{:S(2)}, u32[]{:S(2)}) async-start(bf16[64,8,512]{2,0,1:T(8,128)(2,1)} %bitcast.10), calls=%async_computation.1 | async-start | bytes 1048576 | tf_op jit(solution)/shard_map/all_to_all | solution.py:40
  77.6 10.3 %all-to-all-done.1 = bf16[64,8,512]{2,0,1:T(8,128)(2,1)S(1)} async-done(((bf16[64,8,512]{2,0,1:T(8,128)(2,1)}), bf16[64,8,512]{2,0,1:T(8,128)(2,1)S(1)}, u32[]{:S(2)}, u32[]{:S(2)}) %all-to-all-start.1) | async-done | bytes 524320 | tf_op jit(solution)/shard_map/all_to_all | solution.py:40
  89.5 3.8 %all-to-all-start.7 = ((bf16[64,8,2048]{2,0,1:T(8,128)(2,1)}), bf16[64,8,2048]{2,0,1:T(8,128)(2,1)S(1)}, u32[]{:S(2)}, u32[]{:S(2)}) async-start(bf16[64,8,2048]{2,0,1:T(8,128)(2,1)} %bitcast.65), calls=%async_computation.7 | async-start | bytes 4194304 | tf_op jit(solution)/shard_map/all_to_all | solution.py:118
  114.6 2.5 scatter-add.34
  121.4 2.4 fusion.17
  126.1 2.4 fusion.24
  133.6 2.5 fusion.26
  136.2 3.9 %copy.167 = bf16[1024,4,128]{2,1,0:T(4,128)(2,1)} copy(f32[1024,4,128]{2,0,1:T(8,128)} %fusion.26) | data formatting | bytes 3145728 | tf_op jit(solution)/shard_map/scatter-add | solution.py:97
  141.6 3.0 %fusion.60 = (bf16[512,1,512]{2,1,0:T(2,128)(2,1)S(1)}, f32[512,1,512]{2,1,0:T(1,128)}) fusion(pred[]{:T(512)S(6)} %eq.5, bf16[512,2,512]{2,1,0:T(2,128)(2,1)S(1)} %reshape.498), kind=kLoop, calls=%fused_computation.98 | loop fusion | flops 786432 | bytes 2621441 | tf_op jit(solution)/shard_map/convert_element_type | solution.py:106
  146.0 2.4 fusion.54
  150.4 2.7 %fusion.53 = bf16[128,4,128]{2,0,1:T(8,128)(2,1)} fusion(f32[4,128,256]{1,2,0:T(8,128)} %convolution_bitcast_fusion.9, bf16[256,4,128]{2,1,0:T(4,128)(2,1)} %copy-done.18, f32[4,128,256]{1,2,0:T(8,128)} %get-tuple-element.129, f32[4,128]{1,0:T(4,128)S(1)} %get-tuple-element.128), kind=kOutput, calls=%fused_computation.91 | convolution fusion | flops 34538240 | bytes 1443840 | tf_op jit(solution)/shard_map/hqk,khd->qhd/dot_general | solution.py:90
  154.2 2.7 %fusion.52 = bf16[128,4,128]{2,0,1:T(8,128)(2,1)} fusion(f32[4,128,256]{1,2,0:T(8,128)} %convolution_bitcast_fusion.10, bf16[256,4,128]{2,1,0:T(4,128)(2,1)} %slice.311, f32[4,128,256]{1,2,0:T(8,128)} %get-tuple-element.131, f32[4,128]{1,0:T(4,128)S(1)} %get-tuple-element.130), kind=kOutput, calls=%fused_computation.90 | convolution fusion | flops 34538240 | bytes 1443840 | tf_op jit(solution)/shard_map/hqk,khd->qhd/dot_general | solution.py:90
  160.3 2.4 convolution_bitcast_fusion.7
  162.7 2.6 %scatter-add.26 = f32[1024,4,128]{2,0,1:T(8,128)} pad(f32[256,4,128]{2,0,1:T(8,128)} %convolution_bitcast_fusion.7, f32[]{:T(128)} %constant.216.clone.1), padding=0_768x0_0x0_0 | pad | bytes 2621444 | tf_op jit(solution)/shard_map/scatter-add | solution.py:94
  165.3 2.8 %fusion.18 = f32[1024,4,128]{2,0,1:T(8,128)} fusion(f32[1024,4,128]{2,0,1:T(8,128)} %scatter-add.26, f32[4,128,256]{1,2,0:T(8,128)} %convolution_bitcast_fusion.10, bf16[128,4,128]{2,1,0:T(4,128)(2,1)S(1)} %copy-done.23, f32[4,128,256]{1,2,0:T(8,128)} %get-tuple-element.131, f32[4,128]{1,0:T(4,128)S(1)} %get-tuple-element.130), kind=kOutput, calls=%fused_computation.43 | convolution fusion | flops 34472704 | bytes 2756608 | tf_op jit(solution)/shard_map/hqk,qhd->khd/dot_general | solution.py:95
  170.1 4.8 %all-to-all-start.4 = ((bf16[8,64,1,512]{3,1,2,0:T(8,128)(2,1)}), bf16[8,64,1,512]{3,1,2,0:T(8,128)(2,1)}, u32[]{:S(2)}, u32[]{:S(2)}) async-start(bf16[8,64,1,512]{3,1,2,0:T(8,128)(2,1)} %bitcast.239), calls=%async_computation.4 | async-start | bytes 1048576 | tf_op jit(solution)/shard_map/all_to_all | solution.py:142
  174.9 2.3 fusion.241
  181.4 2.9 %copy.181 = f32[2048,1,256]{2,0,1:T(8,128)} copy(f32[2048,1,256]{0,2,1:T(8,128)} %get-tuple-element.100) | data formatting | bytes 4194304
  187.7 2.8 %fusion.20 = f32[1024,4,128]{2,0,1:T(8,128)} fusion(f32[1024,4,128]{2,0,1:T(8,128)} %fusion.18, f32[4,128,256]{1,2,0:T(8,128)} %convolution_bitcast_fusion.9, bf16[128,4,128]{2,1,0:T(4,128)(2,1)S(1)} %copy-done.22, f32[4,128,256]{1,2,0:T(8,128)} %get-tuple-element.129, f32[4,128]{1,0:T(4,128)S(1)} %get-tuple-element.128), kind=kOutput, calls=%fused_computation.50 | convolution fusion | flops 34603776 | bytes 3280896 | tf_op jit(solution)/shard_map/hqk,qhd->khd/dot_general | solution.py:95
  190.5 2.8 %fusion.22 = f32[1024,4,128]{2,0,1:T(8,128)} fusion(f32[1024,4,128]{2,0,1:T(8,128)} %fusion.20, f32[4,128,256]{1,2,0:T(8,128)} %copy-done.7, bf16[128,4,128]{2,1,0:T(4,128)(2,1)S(1)} %copy-done.20, f32[4,128,256]{1,2,0:T(8,128)} %get-tuple-element.127, f32[4,128]{1,0:T(4,128)S(1)} %get-tuple-element.126), kind=kOutput, calls=%fused_computation.52 | convolution fusion | flops 34603776 | bytes 3280896 | tf_op jit(solution)/shard_map/hqk,qhd->khd/dot_general | solution.py:95
  193.3 3.9 %copy.160 = bf16[1024,4,128]{2,1,0:T(4,128)(2,1)} copy(f32[1024,4,128]{2,0,1:T(8,128)} %fusion.22) | data formatting | bytes 3145728 | tf_op jit(solution)/shard_map/scatter-add | solution.py:94
  198.7 3.0 %fusion.57 = (bf16[512,1,512]{2,1,0:T(2,128)(2,1)S(1)}, f32[512,1,512]{2,1,0:T(1,128)}) fusion(pred[]{:T(512)S(6)} %eq.5, bf16[512,2,512]{2,1,0:T(2,128)(2,1)S(1)} %reshape.494), kind=kLoop, calls=%fused_computation.95 | loop fusion | flops 786432 | bytes 2621441 | tf_op jit(solution)/shard_map/convert_element_type | solution.py:106
  202.7 2.7 %fusion.8 = bf16[2048,256]{1,0:T(8,128)(2,1)} fusion(bf16[2048,256]{1,0:T(8,128)(2,1)} %collective-permute-done.4, f32[2048,1,256]{2,0,1:T(8,128)S(1)} %copy-done, f32[2048,1,256]{2,0,1:T(8,128)S(1)} %copy.182, pred[]{:T(512)S(6)} %eq.5), kind=kLoop, calls=%fused_computation.9 | loop fusion | flops 2097152 | bytes 6291457 | tf_op jit(solution)/shard_map/convert_element_type | solution.py:128
  206.7 19.9 %all_to_all.120 = bf16[8,64,1,512]{3,1,2,0:T(8,128)(2,1)S(1)} all-to-all(bf16[8,64,1,512]{3,1,2,0:T(8,128)(2,1)S(1)} %bitcast.248), channel_id=1, replica_groups=mesh['dp'=4,'seq'=8] {'seq'}, dimensions={0} | all-to-all | bytes 1048576 | tf_op jit(solution)/shard_map/all_to_all | solution.py:143
  226.6 3.8 %all-to-all-start.6 = ((bf16[8,64,1,512]{3,1,2,0:T(8,128)(2,1)}), bf16[8,64,1,512]{3,1,2,0:T(8,128)(2,1)S(1)}, u32[]{:S(2)}, u32[]{:S(2)}) async-start(bf16[8,64,1,512]{3,1,2,0:T(8,128)(2,1)} %bitcast.60), calls=%async_computation.6 | async-start | bytes 1048576 | tf_op jit(solution)/shard_map/all_to_all | solution.py:144
  234.6 10.8 %all-to-all-done.6 = bf16[8,64,1,512]{3,1,2,0:T(8,128)(2,1)S(1)} async-done(((bf16[8,64,1,512]{3,1,2,0:T(8,128)(2,1)}), bf16[8,64,1,512]{3,1,2,0:T(8,128)(2,1)S(1)}, u32[]{:S(2)}, u32[]{:S(2)}) %all-to-all-start.6) | async-done | bytes 524320 | tf_op jit(solution)/shard_map/all_to_all | solution.py:144
  (150 shorter events, 76.6 us)
Async XLA Ops:
  7.2 8.9 %copy-start.12 = (bf16[1,128,2048]{2,1,0:T(8,128)(2,1)S(1)}, bf16[1,128,2048]{2,1,0:T(8,128)(2,1)}, u32[]{:S(2)}) copy-start(bf16[1,128,2048]{2,1,0:T(8,128)(2,1)} %param.24) | copy-start | bytes 1572868
  9.6 25.5 %copy-start.13 = (bf16[1,128,2048]{2,1,0:T(8,128)(2,1)S(1)}, bf16[1,128,2048]{2,1,0:T(8,128)(2,1)}, u32[]{:S(2)}) copy-start(bf16[1,128,2048]{2,1,0:T(8,128)(2,1)} %param.22) | copy-start | bytes 1572868
  9.6 21.8 %all-to-all-start.2 = ((bf16[64,8,512]{2,0,1:T(8,128)(2,1)}), bf16[64,8,512]{2,0,1:T(8,128)(2,1)S(1)}, u32[]{:S(2)}, u32[]{:S(2)}) async-start(bf16[64,8,512]{2,0,1:T(8,128)(2,1)} %bitcast.15), calls=%async_computation.2 | async-start | bytes 1048576 | tf_op jit(solution)/shard_map/all_to_all | solution.py:42
  31.4 22.4 %copy-start.14 = (bf16[1,128,2048]{2,1,0:T(8,128)(2,1)S(1)}, bf16[1,128,2048]{2,1,0:T(8,128)(2,1)}, u32[]{:S(2)}) copy-start(bf16[1,128,2048]{2,1,0:T(8,128)(2,1)} %param.21) | copy-start | bytes 1572868
  31.4 18.9 %all-to-all-start.3 = ((bf16[64,8,512]{2,0,1:T(8,128)(2,1)}), bf16[64,8,512]{2,0,1:T(8,128)(2,1)S(1)}, u32[]{:S(2)}, u32[]{:S(2)}) async-start(bf16[64,8,512]{2,0,1:T(8,128)(2,1)} %bitcast.24), calls=%async_computation.3 | async-start | bytes 1048576 | tf_op jit(solution)/shard_map/all_to_all | solution.py:43
  50.4 18.8 %all-to-all-start = ((bf16[64,8,512]{2,0,1:T(8,128)(2,1)}), bf16[64,8,512]{2,0,1:T(8,128)(2,1)S(1)}, u32[]{:S(2)}, u32[]{:S(2)}) async-start(bf16[64,8,512]{2,0,1:T(8,128)(2,1)} %bitcast.1), calls=%async_computation | async-start | bytes 1048576 | tf_op jit(solution)/shard_map/all_to_all | solution.py:41
  69.1 18.8 %all-to-all-start.1 = ((bf16[64,8,512]{2,0,1:T(8,128)(2,1)}), bf16[64,8,512]{2,0,1:T(8,128)(2,1)S(1)}, u32[]{:S(2)}, u32[]{:S(2)}) async-start(bf16[64,8,512]{2,0,1:T(8,128)(2,1)} %bitcast.10), calls=%async_computation.1 | async-start | bytes 1048576 | tf_op jit(solution)/shard_map/all_to_all | solution.py:40
  74.1 30.5 %collective-permute-start = (bf16[512,512]{1,0:T(8,128)(2,1)S(1)}, bf16[512,512]{1,0:T(8,128)(2,1)}, u32[]{:S(2)}, u32[]{:S(2)}) collective-permute-start(bf16[512,512]{1,0:T(8,128)(2,1)S(1)} %bitcast.238), channel_id=1, source_target_pairs={{0,1},{1,0},{2,3},{3,2},{4,5},{5,4},{6,7},{7,6},{8,9},{9,8},{10,11... | collective-permute-start | bytes 1572872 | tf_op jit(solution)/shard_map/ppermute | solution.py:10
  76.6 51.8 %collective-permute-start.1 = (bf16[512,512]{1,0:T(8,128)(2,1)S(1)}, bf16[512,512]{1,0:T(8,128)(2,1)}, u32[]{:S(2)}, u32[]{:S(2)}) collective-permute-start(bf16[512,512]{1,0:T(8,128)(2,1)S(1)} %bitcast.237), channel_id=1, source_target_pairs={{0,1},{1,0},{2,3},{3,2},{4,5},{5,4},{6,7},{7,6},{8,9},{9,8},{10,11... | collective-permute-start | bytes 1572872 | tf_op jit(solution)/shard_map/ppermute | solution.py:10
  89.5 80.6 %all-to-all-start.7 = ((bf16[64,8,2048]{2,0,1:T(8,128)(2,1)}), bf16[64,8,2048]{2,0,1:T(8,128)(2,1)S(1)}, u32[]{:S(2)}, u32[]{:S(2)}) async-start(bf16[64,8,2048]{2,0,1:T(8,128)(2,1)} %bitcast.65), calls=%async_computation.7 | async-start | bytes 4194304 | tf_op jit(solution)/shard_map/all_to_all | solution.py:118
  110.1 6.9 %copy-start.15 = (bf16[256,4,128]{2,1,0:T(4,128)(2,1)}, bf16[256,4,128]{2,1,0:T(4,128)(2,1)S(1)}, u32[]{:S(2)}) copy-start(bf16[256,4,128]{2,1,0:T(4,128)(2,1)S(1)} %slice.303) | copy-start | bytes 786436
  112.3 4.8 %copy-start.19 = (bf16[128,4,128]{2,1,0:T(4,128)(2,1)S(1)}, bf16[128,4,128]{2,1,0:T(4,128)(2,1)}, u32[]{:S(2)}) copy-start(bf16[128,4,128]{2,1,0:T(4,128)(2,1)} %slice.329) | copy-start | bytes 393220
  117.1 4.3 %copy-start.9 = (bf16[128,4,128]{2,1,0:T(4,128)(2,1)S(1)}, bf16[128,4,128]{2,1,0:T(4,128)(2,1)}, u32[]{:S(2)}) copy-start(bf16[128,4,128]{2,1,0:T(4,128)(2,1)} %slice.317) | copy-start | bytes 393220
  121.4 4.7 %copy-start.11 = (bf16[128,4,128]{2,1,0:T(4,128)(2,1)S(1)}, bf16[128,4,128]{2,1,0:T(4,128)(2,1)}, u32[]{:S(2)}) copy-start(bf16[128,4,128]{2,1,0:T(4,128)(2,1)} %slice.325) | copy-start | bytes 393220
  124.2 4.3 %copy-start.18 = (bf16[256,4,128]{2,1,0:T(4,128)(2,1)}, bf16[256,4,128]{2,1,0:T(4,128)(2,1)S(1)}, u32[]{:S(2)}) copy-start(bf16[256,4,128]{2,1,0:T(4,128)(2,1)S(1)} %slice.319) | copy-start | bytes 786436
  141.5 4.2 %copy-start.6 = (bf16[256,4,128]{2,1,0:T(4,128)(2,1)S(1)}, bf16[256,4,128]{2,1,0:T(4,128)(2,1)}, u32[]{:S(2)}) copy-start(bf16[256,4,128]{2,1,0:T(4,128)(2,1)} %slice.331) | copy-start | bytes 786436
  145.5 22.5 %collective-permute-start.3 = (bf16[512,512]{1,0:T(8,128)(2,1)}, bf16[512,512]{1,0:T(8,128)(2,1)}, u32[]{:S(2)}, u32[]{:S(2)}) collective-permute-start(bf16[512,512]{1,0:T(8,128)(2,1)} %bitcast.233), channel_id=1, source_target_pairs={{0,1},{1,0},{2,3},{3,2},{4,5},{5,4},{6,7},{7,6},{8,9},{9,8},{10,11... | collective-permute-start | bytes 1572872 | tf_op jit(solution)/shard_map/ppermute | solution.py:10
  146.0 7.2 %copy-start.7 = (f32[4,128,256]{1,2,0:T(8,128)}, f32[4,128,256]{1,2,0:T(8,128)S(1)}, u32[]{:S(2)}) copy-start(f32[4,128,256]{1,2,0:T(8,128)S(1)} %convolution_bitcast_fusion.8) | copy-start | bytes 1572868
  148.5 4.7 %copy-start.4 = (bf16[256,4,128]{2,1,0:T(4,128)(2,1)S(1)}, bf16[256,4,128]{2,1,0:T(4,128)(2,1)}, u32[]{:S(2)}) copy-start(bf16[256,4,128]{2,1,0:T(4,128)(2,1)} %slice.315) | copy-start | bytes 786436
  148.5 4.7 %copy-start.10 = (bf16[128,4,128]{2,1,0:T(4,128)(2,1)S(1)}, bf16[128,4,128]{2,1,0:T(4,128)(2,1)}, u32[]{:S(2)}) copy-start(bf16[128,4,128]{2,1,0:T(4,128)(2,1)} %slice.317) | copy-start | bytes 393220
  153.2 3.8 %copy-start.8 = (bf16[128,4,128]{2,1,0:T(4,128)(2,1)S(1)}, bf16[128,4,128]{2,1,0:T(4,128)(2,1)}, u32[]{:S(2)}) copy-start(bf16[128,4,128]{2,1,0:T(4,128)(2,1)} %slice.309) | copy-start | bytes 393220
  154.2 3.0 %copy-start.16 = (bf16[256,4,128]{2,1,0:T(4,128)(2,1)S(1)}, bf16[256,4,128]{2,1,0:T(4,128)(2,1)}, u32[]{:S(2)}) copy-start(bf16[256,4,128]{2,1,0:T(4,128)(2,1)} %copy-done.15) | copy-start | bytes 786436
  160.3 5.0 %copy-start.23 = (bf16[128,4,128]{2,1,0:T(4,128)(2,1)S(1)}, bf16[128,4,128]{2,1,0:T(4,128)(2,1)}, u32[]{:S(2)}) copy-start(bf16[128,4,128]{2,1,0:T(4,128)(2,1)} %slice.313) | copy-start | bytes 393220
  162.7 5.4 %copy-start.1 = (f32[512,1,512]{2,1,0:T(1,128)S(1)}, f32[512,1,512]{2,1,0:T(1,128)}, u32[]{:S(2)}) copy-start(f32[512,1,512]{2,1,0:T(1,128)} %get-tuple-element.103) | copy-start | bytes 3145732
  170.1 36.5 %all-to-all-start.4 = ((bf16[8,64,1,512]{3,1,2,0:T(8,128)(2,1)}), bf16[8,64,1,512]{3,1,2,0:T(8,128)(2,1)}, u32[]{:S(2)}, u32[]{:S(2)}) async-start(bf16[8,64,1,512]{3,1,2,0:T(8,128)(2,1)} %bitcast.239), calls=%async_computation.4 | async-start | bytes 1048576 | tf_op jit(solution)/shard_map/all_to_all | solution.py:142
  174.9 72.1 %reduce-scatter.2.cloned.1.call-start = ((), (), s32[]{:S(2)}) async-start(), calls=%async_computation.9 | async-start | bytes 1310720 | tf_op jit(solution)/shard_map/reduce_scatter | solution.py:127
  184.4 3.3 %copy-start.22 = (bf16[128,4,128]{2,1,0:T(4,128)(2,1)S(1)}, bf16[128,4,128]{2,1,0:T(4,128)(2,1)}, u32[]{:S(2)}) copy-start(bf16[128,4,128]{2,1,0:T(4,128)(2,1)} %slice.321) | copy-start | bytes 393220
  185.6 4.9 %copy-start.20 = (bf16[128,4,128]{2,1,0:T(4,128)(2,1)S(1)}, bf16[128,4,128]{2,1,0:T(4,128)(2,1)}, u32[]{:S(2)}) copy-start(bf16[128,4,128]{2,1,0:T(4,128)(2,1)} %slice.329) | copy-start | bytes 393220
  185.6 17.1 %collective-permute-start.4 = (bf16[2048,256]{1,0:T(8,128)(2,1)}, bf16[2048,256]{1,0:T(8,128)(2,1)}, u32[]{:S(2)}, u32[]{:S(2)}) collective-permute-start(bf16[2048,256]{1,0:T(8,128)(2,1)} %fusion.61), channel_id=1, source_target_pairs={{0,1},{1,0},{2,3},{3,2},{4,5},{5,4},{6,7},{7,6},{8,9},{9,8},{10,11... | collective-permute-start | bytes 3145736 | tf_op jit(solution)/shard_map/ppermute | solution.py:10
  198.7 3.9 %copy-start = (f32[2048,1,256]{2,0,1:T(8,128)S(1)}, f32[2048,1,256]{2,0,1:T(8,128)}, u32[]{:S(2)}) copy-start(f32[2048,1,256]{2,0,1:T(8,128)} %copy.181) | copy-start | bytes 6291460
  202.7 2.8 %collective-permute-start.2 = (bf16[512,512]{1,0:T(8,128)(2,1)}, bf16[512,512]{1,0:T(8,128)(2,1)}, u32[]{:S(2)}, u32[]{:S(2)}) collective-permute-start(bf16[512,512]{1,0:T(8,128)(2,1)} %bitcast.234), channel_id=1, source_target_pairs={{0,1},{1,0},{2,3},{3,2},{4,5},{5,4},{6,7},{7,6},{8,9},{9,8},{10,11... | collective-permute-start | bytes 1572872 | tf_op jit(solution)/shard_map/ppermute | solution.py:10
  226.6 18.8 %all-to-all-start.6 = ((bf16[8,64,1,512]{3,1,2,0:T(8,128)(2,1)}), bf16[8,64,1,512]{3,1,2,0:T(8,128)(2,1)S(1)}, u32[]{:S(2)}, u32[]{:S(2)}) async-start(bf16[8,64,1,512]{3,1,2,0:T(8,128)(2,1)} %bitcast.60), calls=%async_computation.6 | async-start | bytes 1048576 | tf_op jit(solution)/shard_map/all_to_all | solution.py:144
  (9 other events, 18.4 us)
Sparse Core Ops, SparseCore 0:
  205.5 28.9 reduce-scatter.1
where the time goes:
time: 258 us; the launch traced here: 256 us
  waiting for transfers between devices  62.4 us (24%)
  local copies, waits for them, and re-layouts  61.6 us (24%)
  matrix products  44 us (17%)
  starting transfers between devices  32.3 us (13%)
  other arithmetic  21 us (8%)
  blocking collectives  19.9 us (8%)
  between operations  14.5 us (6%)
    all_to_all x1, blocking collectives, body(): lax.all_to_all(to_tokens(key_grad), 'seq', split_axis=0, concat_axis=2, t...  19.9 us
    all_to_all x1, waiting for transfers between devices, body(): lax.all_to_all(to_heads(values), 'seq', split_axis=1, concat_axis=0, tile...  14 us
    all_to_all x1, waiting for transfers between devices, body(): lax.all_to_all(to_heads(out_grad), 'seq', split_axis=1, concat_axis=0, ti...  13.9 us
    all_to_all x1, waiting for transfers between devices, body(): lax.all_to_all(to_heads(key_vectors), 'seq', split_axis=1, concat_axis=0,...  13.2 us
    dot_general x4, matrix products, body(): jnp.einsum('hqk,qhd->khd', dscore, query_block, preferred_element_type=jn...  10.8 us
    all_to_all x1, waiting for transfers between devices, body(): lax.all_to_all(to_tokens(value_grad), 'seq', split_axis=0, concat_axis=2,...  10.8 us
    all_to_all x1, waiting for transfers between devices, body(): lax.all_to_all(to_heads(queries), 'seq', split_axis=1, concat_axis=0, til...  10.3 us
    dot_general x4, matrix products, body(): jnp.einsum('hqk,qhd->khd', probs_low, grad_block, preferred_element_type=...  9.58 us
  transfers between devices with their start and end apart: 13, of which 5 were waited for; matrix products, arithmetic and copies ran while one was open for 48% of the time, Pallas kernels for 0%

commit v1 on v0

--- a/solution.py
+++ b/solution.py
@@ -141,7 +141,15 @@
     returned = (
         lax.all_to_all(to_tokens(query_grad), "seq", split_axis=0, concat_axis=2, tiled=True),
         lax.all_to_all(to_tokens(key_grad), "seq", split_axis=0, concat_axis=2, tiled=True),
-        lax.all_to_all(to_tokens(value_grad), "seq", split_axis=0, concat_axis=2, tiled=True),
+        jnp.concatenate(
+            lax.all_to_all(
+                jnp.stack(jnp.split(to_tokens(value_grad), lax.axis_size("seq"), axis=0)),
+                "seq",
+                0,
+                0,
+            ),
+            axis=2,
+        ),
     )
     return (from_heads(returned[0]), from_heads(returned[1]), from_heads(returned[2]), weight_grad)
 

time: 258 us -> 236 us (0.915)
  waiting for transfers between devices: 62.4 us -> 84 us
  blocking collectives: 19.9 us -> 0 us
  local copies, waits for them, and re-layouts: 61.6 us -> 48.9 us
  matrix products: 44 us -> 32.1 us
  starting transfers between devices: 32.3 us -> 36.5 us
    all_to_all x1 -> x0, blocking collectives: 19.9 us -> none  [body(): lax.all_to_all(to_tokens(key_grad), 'seq', split_axis=0, concat_axis=2, t...]
    all_to_all x1 -> x2, waiting for transfers between devices: 10.8 us -> 24 us  [the longest x1 12.2 us: body(): lax.all_to_all(to_tokens(key_grad), 'seq', split_axis=0, concat_axis=2, t...]
    all_to_all x1, waiting for transfers between devices: 0.01 us -> 8.39 us  [body(): lax.all_to_all(to_tokens(query_grad), 'seq', split_axis=0, concat_axis=2,...]
    slice x5, local copies, waits for them, and re-layouts: 8.26 us -> 2.78 us  [body(): query_block = query_heads[start:stop]]
    unnamed x60 -> x55, local copies, waits for them, and re-layouts: 6.83 us -> 12.3 us
    dot_general x4, matrix products: 10.8 us -> 6.24 us  [body(): jnp.einsum('hqk,qhd->khd', dscore, query_block, preferred_element_type=jn...]
    scatter-add x2, local copies, waits for them, and re-layouts: 6.51 us -> 2.53 us  [body(): key_total.at[low:high]]
    all_to_all x1 -> x2, starting transfers between devices: 3.75 us -> 7.25 us  [the longest x1 3.75 us: body(): lax.all_to_all(jnp.stack(jnp.split(to_tokens(value_grad), lax.axis_size('...]
  transfers between devices with their start and end apart: 13 -> 14, of which waited for: 5 -> 7; matrix products, arithmetic and copies ran while one was open for 48% -> 40% of each run, Pallas kernels for 0% -> 0%
where the time goes in v1:
time: 236 us; the launch traced here: 235 us
  waiting for transfers between devices  84 us (36%)
  local copies, waits for them, and re-layouts  48.9 us (21%)
  starting transfers between devices  36.5 us (15%)
  matrix products  32.1 us (14%)
  other arithmetic  18.6 us (8%)
  between operations  14.7 us (6%)
    all_to_all x1, waiting for transfers between devices, body(): lax.all_to_all(to_heads(values), 'seq', split_axis=1, concat_axis=0, tile...  14 us
    all_to_all x1, waiting for transfers between devices, body(): lax.all_to_all(to_heads(out_grad), 'seq', split_axis=1, concat_axis=0, ti...  13.9 us
    all_to_all x1, waiting for transfers between devices, body(): lax.all_to_all(to_heads(key_vectors), 'seq', split_axis=1, concat_axis=0,...  13.2 us
    unnamed x55, local copies, waits for them, and re-layouts  12.3 us
    all_to_all x1, waiting for transfers between devices, body(): lax.all_to_all(to_tokens(key_grad), 'seq', split_axis=0, concat_axis=2, t...  12.2 us
    all_to_all x1, waiting for transfers between devices, body(): lax.all_to_all(jnp.stack(jnp.split(to_tokens(value_grad), lax.axis_size('...  11.8 us
    all_to_all x1, waiting for transfers between devices, body(): lax.all_to_all(to_heads(queries), 'seq', split_axis=1, concat_axis=0, til...  10.4 us
    all_to_all x1, waiting for transfers between devices, body(): lax.all_to_all(to_tokens(query_grad), 'seq', split_axis=0, concat_axis=2,...  8.39 us
  transfers between devices with their start and end apart: 14, of which 7 were waited for; matrix products, arithmetic and copies ran while one was open for 40% of the time, Pallas kernels for 0%

profile of v1, /device:TPU:0, one launch (start us, length us, event | category | flops | bytes accessed | tf_op | source)
XLA Modules:
  0.0 234.8 jit_solution(16852492152801601704)
XLA Ops:
  9.6 6.5 %all-to-all-start.2 = ((bf16[64,8,512]{2,0,1:T(8,128)(2,1)}), bf16[64,8,512]{2,0,1:T(8,128)(2,1)S(1)}, u32[]{:S(2)}, u32[]{:S(2)}) async-start(bf16[64,8,512]{2,0,1:T(8,128)(2,1)} %bitcast.15), calls=%async_computation.2 | async-start | bytes 1048576 | tf_op jit(solution)/shard_map/all_to_all | solution.py:42
  17.4 14.0 %all-to-all-done.2 = bf16[64,8,512]{2,0,1:T(8,128)(2,1)S(1)} async-done(((bf16[64,8,512]{2,0,1:T(8,128)(2,1)}), bf16[64,8,512]{2,0,1:T(8,128)(2,1)S(1)}, u32[]{:S(2)}, u32[]{:S(2)}) %all-to-all-start.2) | async-done | bytes 524320 | tf_op jit(solution)/shard_map/all_to_all | solution.py:42
  31.4 3.6 %all-to-all-start.3 = ((bf16[64,8,512]{2,0,1:T(8,128)(2,1)}), bf16[64,8,512]{2,0,1:T(8,128)(2,1)S(1)}, u32[]{:S(2)}, u32[]{:S(2)}) async-start(bf16[64,8,512]{2,0,1:T(8,128)(2,1)} %bitcast.24), calls=%async_computation.3 | async-start | bytes 1048576 | tf_op jit(solution)/shard_map/all_to_all | solution.py:43
  36.4 13.9 %all-to-all-done.3 = bf16[64,8,512]{2,0,1:T(8,128)(2,1)S(1)} async-done(((bf16[64,8,512]{2,0,1:T(8,128)(2,1)}), bf16[64,8,512]{2,0,1:T(8,128)(2,1)S(1)}, u32[]{:S(2)}, u32[]{:S(2)}) %all-to-all-start.3) | async-done | bytes 524320 | tf_op jit(solution)/shard_map/all_to_all | solution.py:43
  50.4 3.5 %all-to-all-start = ((bf16[64,8,512]{2,0,1:T(8,128)(2,1)}), bf16[64,8,512]{2,0,1:T(8,128)(2,1)S(1)}, u32[]{:S(2)}, u32[]{:S(2)}) async-start(bf16[64,8,512]{2,0,1:T(8,128)(2,1)} %bitcast.1), calls=%async_computation | async-start | bytes 1048576 | tf_op jit(solution)/shard_map/all_to_all | solution.py:41
  55.9 13.2 %all-to-all-done = bf16[64,8,512]{2,0,1:T(8,128)(2,1)S(1)} async-done(((bf16[64,8,512]{2,0,1:T(8,128)(2,1)}), bf16[64,8,512]{2,0,1:T(8,128)(2,1)S(1)}, u32[]{:S(2)}, u32[]{:S(2)}) %all-to-all-start) | async-done | bytes 524320 | tf_op jit(solution)/shard_map/all_to_all | solution.py:41
  69.1 3.5 %all-to-all-start.1 = ((bf16[64,8,512]{2,0,1:T(8,128)(2,1)}), bf16[64,8,512]{2,0,1:T(8,128)(2,1)S(1)}, u32[]{:S(2)}, u32[]{:S(2)}) async-start(bf16[64,8,512]{2,0,1:T(8,128)(2,1)} %bitcast.10), calls=%async_computation.1 | async-start | bytes 1048576 | tf_op jit(solution)/shard_map/all_to_all | solution.py:40
  77.6 10.4 %all-to-all-done.1 = bf16[64,8,512]{2,0,1:T(8,128)(2,1)S(1)} async-done(((bf16[64,8,512]{2,0,1:T(8,128)(2,1)}), bf16[64,8,512]{2,0,1:T(8,128)(2,1)S(1)}, u32[]{:S(2)}, u32[]{:S(2)}) %all-to-all-start.1) | async-done | bytes 524320 | tf_op jit(solution)/shard_map/all_to_all | solution.py:40
  89.5 4.5 %all-to-all-start.7 = ((bf16[64,8,2048]{2,0,1:T(8,128)(2,1)}), bf16[64,8,2048]{2,0,1:T(8,128)(2,1)}, u32[]{:S(2)}, u32[]{:S(2)}) async-start(bf16[64,8,2048]{2,0,1:T(8,128)(2,1)} %bitcast.70), calls=%async_computation.7 | async-start | bytes 4194304 | tf_op jit(solution)/shard_map/all_to_all | solution.py:118
  110.1 2.1 fusion.229
  112.2 2.1 fusion.234
  114.3 2.2 fusion.239
  119.8 1.9 fusion.22
  124.0 2.2 convolution_bitcast_fusion.3
  132.0 2.3 copy.167
  135.8 2.2 fusion.60
  139.2 3.0 %fusion.57 = (bf16[512,1,512]{2,1,0:T(2,128)(2,1)S(1)}, f32[512,1,512]{2,1,0:T(1,128)}) fusion(pred[]{:T(512)S(6)} %eq.5, bf16[512,2,512]{2,1,0:T(2,128)(2,1)S(1)} %reshape.507), kind=kLoop, calls=%fused_computation.95 | loop fusion | flops 786432 | bytes 2621441 | tf_op jit(solution)/shard_map/convert_element_type | solution.py:106
  142.2 1.9 fusion.54
  147.3 2.0 fusion.52
  150.5 2.9 %fusion.249 = f32[512,2048]{1,0:T(8,128)S(1)} fusion(bf16[512,512]{1,0:T(8,128)(2,1)S(1)} %fusion.62, bf16[512,2048]{1,0:T(8,128)(2,1)} %bitcast.73), kind=kOutput, calls=%fused_computation.237 | convolution fusion | flops 1073741824 | bytes 6815744 | tf_op jit(solution)/shard_map/td,tc->dc/dot_general | solution.py:121
  153.4 2.2 fusion.226
  155.7 1.9 copy.181
  157.6 3.0 %copy.180 = f32[2048,1,256]{2,0,1:T(8,128)} copy(f32[2048,1,256]{0,2,1:T(8,128)} %get-tuple-element.100) | data formatting | bytes 4194304
  163.5 1.9 fusion.51
  166.9 4.8 %all-to-all-start.4 = ((bf16[8,64,1,512]{3,1,2,0:T(8,128)(2,1)}), bf16[8,64,1,512]{3,1,2,0:T(8,128)(2,1)S(1)}, u32[]{:S(2)}, u32[]{:S(2)}) async-start(bf16[8,64,1,512]{3,1,2,0:T(8,128)(2,1)} %bitcast.268), calls=%async_computation.4 | async-start | bytes 1048576 | tf_op jit(solution)/shard_map/all_to_all | solution.py:142
  172.4 2.4 %fusion.63 = bf16[512,512]{1,0:T(8,128)(2,1)} fusion(f32[512,1,512]{2,1,0:T(1,128)} %get-tuple-element.105, bf16[512,512]{1,0:T(8,128)(2,1)} %collective-permute-done.2), kind=kLoop, calls=%fused_computation.103 | loop fusion | flops 786432 | bytes 2097152 | tf_op jit(solution)/shard_map/convert_element_type | solution.py:111
  175.4 2.6 %fusion.8 = bf16[2048,256]{1,0:T(8,128)(2,1)} fusion(bf16[2048,256]{1,0:T(8,128)(2,1)} %collective-permute-done.4, f32[2048,1,256]{2,0,1:T(8,128)S(1)} %copy-done, f32[2048,1,256]{2,0,1:T(8,128)S(1)} %copy.181, pred[]{:T(512)S(6)} %eq.5), kind=kLoop, calls=%fused_computation.9 | loop fusion | flops 2097152 | bytes 6291457 | tf_op jit(solution)/shard_map/convert_element_type | solution.py:128
  178.7 8.4 %all-to-all-done.4 = bf16[8,64,1,512]{3,1,2,0:T(8,128)(2,1)S(1)} async-done(((bf16[8,64,1,512]{3,1,2,0:T(8,128)(2,1)}), bf16[8,64,1,512]{3,1,2,0:T(8,128)(2,1)S(1)}, u32[]{:S(2)}, u32[]{:S(2)}) %all-to-all-start.4) | async-done | bytes 524320 | tf_op jit(solution)/shard_map/all_to_all | solution.py:142
  187.1 3.5 %all-to-all-start.5 = ((bf16[8,64,1,512]{3,1,2,0:T(8,128)(2,1)}), bf16[8,64,1,512]{3,1,2,0:T(8,128)(2,1)S(1)}, u32[]{:S(2)}, u32[]{:S(2)}) async-start(bf16[8,64,1,512]{3,1,2,0:T(8,128)(2,1)} %bitcast.275), calls=%async_computation.5 | async-start | bytes 1048576 | tf_op jit(solution)/shard_map/all_to_all | solution.py:143
  193.7 12.2 %all-to-all-done.5 = bf16[8,64,1,512]{3,1,2,0:T(8,128)(2,1)S(1)} async-done(((bf16[8,64,1,512]{3,1,2,0:T(8,128)(2,1)}), bf16[8,64,1,512]{3,1,2,0:T(8,128)(2,1)S(1)}, u32[]{:S(2)}, u32[]{:S(2)}) %all-to-all-start.5) | async-done | bytes 524320 | tf_op jit(solution)/shard_map/all_to_all | solution.py:143
  205.8 3.8 %all-to-all-start.6 = ((bf16[8,1,64,1,512]{4,2,3,1,0:T(8,128)(2,1)}), bf16[8,1,64,1,512]{4,2,3,1,0:T(8,128)(2,1)S(1)}, u32[]{:S(2)}, u32[]{:S(2)}) async-start(bf16[8,1,64,1,512]{4,2,3,1,0:T(8,128)(2,1)} %fusion.126), calls=%async_computation.6 | async-start | bytes 1048576 | tf_op jit(solution)/shard_map/all_to_all | solution.py:145
  212.8 11.8 %all-to-all-done.6 = bf16[8,1,64,1,512]{4,2,3,1,0:T(8,128)(2,1)S(1)} async-done(((bf16[8,1,64,1,512]{4,2,3,1,0:T(8,128)(2,1)}), bf16[8,1,64,1,512]{4,2,3,1,0:T(8,128)(2,1)S(1)}, u32[]{:S(2)}, u32[]{:S(2)}) %all-to-all-start.6) | async-done | bytes 524320 | tf_op jit(solution)/shard_map/all_to_all | solution.py:145
  (147 shorter events, 63.6 us)
Async XLA Ops:
  7.2 8.9 %copy-start.6 = (bf16[1,128,2048]{2,1,0:T(8,128)(2,1)S(1)}, bf16[1,128,2048]{2,1,0:T(8,128)(2,1)}, u32[]{:S(2)}) copy-start(bf16[1,128,2048]{2,1,0:T(8,128)(2,1)} %param.24) | copy-start | bytes 1572868
  9.6 25.5 %copy-start.7 = (bf16[1,128,2048]{2,1,0:T(8,128)(2,1)S(1)}, bf16[1,128,2048]{2,1,0:T(8,128)(2,1)}, u32[]{:S(2)}) copy-start(bf16[1,128,2048]{2,1,0:T(8,128)(2,1)} %param.22) | copy-start | bytes 1572868
  9.6 21.8 %all-to-all-start.2 = ((bf16[64,8,512]{2,0,1:T(8,128)(2,1)}), bf16[64,8,512]{2,0,1:T(8,128)(2,1)S(1)}, u32[]{:S(2)}, u32[]{:S(2)}) async-start(bf16[64,8,512]{2,0,1:T(8,128)(2,1)} %bitcast.15), calls=%async_computation.2 | async-start | bytes 1048576 | tf_op jit(solution)/shard_map/all_to_all | solution.py:42
  31.4 22.4 %copy-start.8 = (bf16[1,128,2048]{2,1,0:T(8,128)(2,1)S(1)}, bf16[1,128,2048]{2,1,0:T(8,128)(2,1)}, u32[]{:S(2)}) copy-start(bf16[1,128,2048]{2,1,0:T(8,128)(2,1)} %param.21) | copy-start | bytes 1572868
  31.4 18.9 %all-to-all-start.3 = ((bf16[64,8,512]{2,0,1:T(8,128)(2,1)}), bf16[64,8,512]{2,0,1:T(8,128)(2,1)S(1)}, u32[]{:S(2)}, u32[]{:S(2)}) async-start(bf16[64,8,512]{2,0,1:T(8,128)(2,1)} %bitcast.24), calls=%async_computation.3 | async-start | bytes 1048576 | tf_op jit(solution)/shard_map/all_to_all | solution.py:43
  50.4 18.8 %all-to-all-start = ((bf16[64,8,512]{2,0,1:T(8,128)(2,1)}), bf16[64,8,512]{2,0,1:T(8,128)(2,1)S(1)}, u32[]{:S(2)}, u32[]{:S(2)}) async-start(bf16[64,8,512]{2,0,1:T(8,128)(2,1)} %bitcast.1), calls=%async_computation | async-start | bytes 1048576 | tf_op jit(solution)/shard_map/all_to_all | solution.py:41
  69.1 18.8 %all-to-all-start.1 = ((bf16[64,8,512]{2,0,1:T(8,128)(2,1)}), bf16[64,8,512]{2,0,1:T(8,128)(2,1)S(1)}, u32[]{:S(2)}, u32[]{:S(2)}) async-start(bf16[64,8,512]{2,0,1:T(8,128)(2,1)} %bitcast.10), calls=%async_computation.1 | async-start | bytes 1048576 | tf_op jit(solution)/shard_map/all_to_all | solution.py:40
  74.1 23.6 %collective-permute-start.1 = (bf16[512,512]{1,0:T(8,128)(2,1)S(1)}, bf16[512,512]{1,0:T(8,128)(2,1)}, u32[]{:S(2)}, u32[]{:S(2)}) collective-permute-start(bf16[512,512]{1,0:T(8,128)(2,1)S(1)} %bitcast.263), channel_id=1, source_target_pairs={{0,1},{1,0},{2,3},{3,2},{4,5},{5,4},{6,7},{7,6},{8,9},{9,8},{10,11... | collective-permute-start | bytes 1572872 | tf_op jit(solution)/shard_map/ppermute | solution.py:10
  76.6 22.7 %collective-permute-start = (bf16[512,512]{1,0:T(8,128)(2,1)S(1)}, bf16[512,512]{1,0:T(8,128)(2,1)S(1)}, u32[]{:S(2)}, u32[]{:S(2)}) collective-permute-start(bf16[512,512]{1,0:T(8,128)(2,1)S(1)} %bitcast.264), channel_id=1, source_target_pairs={{0,1},{1,0},{2,3},{3,2},{4,5},{5,4},{6,7},{7,6},{8,9},{9,8},{10,11... | collective-permute-start | bytes 1572872 | tf_op jit(solution)/shard_map/ppermute | solution.py:10
  89.5 61.1 %all-to-all-start.7 = ((bf16[64,8,2048]{2,0,1:T(8,128)(2,1)}), bf16[64,8,2048]{2,0,1:T(8,128)(2,1)}, u32[]{:S(2)}, u32[]{:S(2)}) async-start(bf16[64,8,2048]{2,0,1:T(8,128)(2,1)} %bitcast.70), calls=%async_computation.7 | async-start | bytes 4194304 | tf_op jit(solution)/shard_map/all_to_all | solution.py:118
  94.0 1.5 copy-start.10
  94.0 2.2 copy-start.9
  104.2 2.2 copy-start.4
  104.6 2.0 copy-start.18
  104.6 2.0 copy-start.20
  104.8 2.1 copy-start.11
  106.1 12.1 %copy-start.3 = (f32[4,128,256]{1,2,0:T(8,128)}, f32[4,128,256]{1,2,0:T(8,128)S(1)}, u32[]{:S(2)}) copy-start(f32[4,128,256]{1,2,0:T(8,128)S(1)} %convolution_bitcast_fusion.9) | copy-start | bytes 1572868
  106.4 10.2 %copy-start.2 = (f32[4,128,256]{1,2,0:T(8,128)}, f32[4,128,256]{1,2,0:T(8,128)S(1)}, u32[]{:S(2)}) copy-start(f32[4,128,256]{1,2,0:T(8,128)S(1)} %convolution_bitcast_fusion.10) | copy-start | bytes 1572868
  118.2 1.6 copy-start.16
  129.0 1.6 copy-start.17
  139.0 3.2 %copy-start.14 = (bf16[256,4,128]{2,1,0:T(4,128)(2,1)S(1)}, bf16[256,4,128]{2,1,0:T(4,128)(2,1)}, u32[]{:S(2)}) copy-start(bf16[256,4,128]{2,1,0:T(4,128)(2,1)} %slice.335) | copy-start | bytes 786436
  139.0 10.3 %collective-permute-start.3 = (bf16[512,512]{1,0:T(8,128)(2,1)}, bf16[512,512]{1,0:T(8,128)(2,1)}, u32[]{:S(2)}, u32[]{:S(2)}) collective-permute-start(bf16[512,512]{1,0:T(8,128)(2,1)} %bitcast.260), channel_id=1, source_target_pairs={{0,1},{1,0},{2,3},{3,2},{4,5},{5,4},{6,7},{7,6},{8,9},{9,8},{10,11... | collective-permute-start | bytes 1572872 | tf_op jit(solution)/shard_map/ppermute | solution.py:10
  142.2 3.2 %copy-start.13 = (bf16[256,4,128]{2,1,0:T(4,128)(2,1)S(1)}, bf16[256,4,128]{2,1,0:T(4,128)(2,1)}, u32[]{:S(2)}) copy-start(bf16[256,4,128]{2,1,0:T(4,128)(2,1)} %slice.327) | copy-start | bytes 786436
  144.1 3.2 %copy-start.15 = (bf16[256,4,128]{2,1,0:T(4,128)(2,1)S(1)}, bf16[256,4,128]{2,1,0:T(4,128)(2,1)}, u32[]{:S(2)}) copy-start(bf16[256,4,128]{2,1,0:T(4,128)(2,1)} %slice.319) | copy-start | bytes 786436
  145.0 27.4 %collective-permute-start.2 = (bf16[512,512]{1,0:T(8,128)(2,1)}, bf16[512,512]{1,0:T(8,128)(2,1)}, u32[]{:S(2)}, u32[]{:S(2)}) collective-permute-start(bf16[512,512]{1,0:T(8,128)(2,1)} %bitcast.261), channel_id=1, source_target_pairs={{0,1},{1,0},{2,3},{3,2},{4,5},{5,4},{6,7},{7,6},{8,9},{9,8},{10,11... | collective-permute-start | bytes 1572872 | tf_op jit(solution)/shard_map/ppermute | solution.py:10
  160.5 3.0 %copy-start.12 = (bf16[256,4,128]{2,1,0:T(4,128)(2,1)S(1)}, bf16[256,4,128]{2,1,0:T(4,128)(2,1)}, u32[]{:S(2)}) copy-start(bf16[256,4,128]{2,1,0:T(4,128)(2,1)} %copy-done.11) | copy-start | bytes 786436
  161.7 13.6 %collective-permute-start.4 = (bf16[2048,256]{1,0:T(8,128)(2,1)}, bf16[2048,256]{1,0:T(8,128)(2,1)}, u32[]{:S(2)}, u32[]{:S(2)}) collective-permute-start(bf16[2048,256]{1,0:T(8,128)(2,1)} %fusion.61), channel_id=1, source_target_pairs={{0,1},{1,0},{2,3},{3,2},{4,5},{5,4},{6,7},{7,6},{8,9},{9,8},{10,11... | collective-permute-start | bytes 3145736 | tf_op jit(solution)/shard_map/ppermute | solution.py:10
  166.9 20.1 %all-to-all-start.4 = ((bf16[8,64,1,512]{3,1,2,0:T(8,128)(2,1)}), bf16[8,64,1,512]{3,1,2,0:T(8,128)(2,1)S(1)}, u32[]{:S(2)}, u32[]{:S(2)}) async-start(bf16[8,64,1,512]{3,1,2,0:T(8,128)(2,1)} %bitcast.268), calls=%async_computation.4 | async-start | bytes 1048576 | tf_op jit(solution)/shard_map/all_to_all | solution.py:142
  171.7 54.5 %reduce-scatter.2.cloned.1.call-start = ((), (), s32[]{:S(2)}) async-start(), calls=%async_computation.9 | async-start | bytes 1310720 | tf_op jit(solution)/shard_map/reduce_scatter | solution.py:127
  171.7 3.6 %copy-start = (f32[2048,1,256]{2,0,1:T(8,128)S(1)}, f32[2048,1,256]{2,0,1:T(8,128)}, u32[]{:S(2)}) copy-start(f32[2048,1,256]{2,0,1:T(8,128)} %copy.180) | copy-start | bytes 6291460
  187.1 18.8 %all-to-all-start.5 = ((bf16[8,64,1,512]{3,1,2,0:T(8,128)(2,1)}), bf16[8,64,1,512]{3,1,2,0:T(8,128)(2,1)S(1)}, u32[]{:S(2)}, u32[]{:S(2)}) async-start(bf16[8,64,1,512]{3,1,2,0:T(8,128)(2,1)} %bitcast.275), calls=%async_computation.5 | async-start | bytes 1048576 | tf_op jit(solution)/shard_map/all_to_all | solution.py:143
  205.8 18.8 %all-to-all-start.6 = ((bf16[8,1,64,1,512]{4,2,3,1,0:T(8,128)(2,1)}), bf16[8,1,64,1,512]{4,2,3,1,0:T(8,128)(2,1)S(1)}, u32[]{:S(2)}, u32[]{:S(2)}) async-start(bf16[8,1,64,1,512]{4,2,3,1,0:T(8,128)(2,1)} %fusion.126), calls=%async_computation.6 | async-start | bytes 1048576 | tf_op jit(solution)/shard_map/all_to_all | solution.py:145
  (4 other events, 3.5 us)
Sparse Core Ops, SparseCore 0:
  178.2 29.1 reduce-scatter.1
